TPU v7x, 32 devices: a whole 2x2x4 slice. The times are simulated.
32 devices in a mesh: grp: 2 (over y), row: 4 (over x, core), col: 4 (over z).
Axes of the slice: x: 2, y: 2, z: 4, core: 2. Of those that a mesh axis runs over, the one named last changes fastest.
Arguments:
- perturbation: bfloat16 [4, 12000, 12000], P('grp', 'row', 'col'), parts along dimension 0, may hold values from -96 to 96
- occ_coeffs: bfloat16 [12000, 2000], P('row', 'col'), may hold values from -0.0546875 to 0.0546875
- vir_coeffs: bfloat16 [12000, 512], P('col', 'row'), may hold values from -0.0546875 to 0.0546875
- occ_energies: float32 [2000], replicated, may hold values from -1 to -0.1
- vir_energies: float32 [512], replicated, may hold values from 0.1 to 1.5
Outputs:
- density_response: bfloat16 [4, 12000, 12000], P('grp', 'row', 'col'), parts along dimension 0
There are 2 independent parts, one for each index of `grp`. A program takes and returns all parts, laid end to end along the dimension named above; an argument that names none is the same for every part. Nothing has to cross between parts.
All inputs are finite; a program needn't handle non-finite values.
Results may differ from a plain program's by a relative error of at most 0.0098.
Values may be sent and summed in bfloat16 or wider, within the bound.
A program may use at most 192 MiB of HBM per device.

v0:
```python
import jax
import jax.numpy as jnp
from jax import lax
from jax.sharding import PartitionSpec as P

BF16 = jnp.bfloat16
F32 = jnp.float32


def per_device(perturbation, occ_coeffs, vir_coeffs, occ_energies, vir_energies):
    vir_rows = lax.all_gather(vir_coeffs, "row", axis=1, tiled=True)
    occ_parts = lax.all_gather(occ_coeffs, "col")
    cols, _, width = occ_parts.shape
    image = jnp.einsum("pij,jv->piv", perturbation, vir_rows, preferred_element_type=F32).astype(
        BF16
    )
    part = jnp.einsum("cio,piv->pcov", occ_parts, image, preferred_element_type=F32).astype(BF16)
    coupling = lax.psum(part, ("row", "col"))
    gaps = occ_energies.reshape(cols, width)[:, :, None] - vir_energies[None, None, :]
    response = (coupling.astype(F32) / gaps[None]).astype(BF16)
    mixed = jnp.einsum("cio,pcov->piv", occ_parts, response, preferred_element_type=F32).astype(
        BF16
    )
    return jnp.einsum("piv,jv->pij", mixed, vir_rows, preferred_element_type=F32).astype(BF16)


def solution(mesh):
    placed = (P("grp", "row", "col"), P("row", "col"), P("col", "row"), P(), P())
    return jax.shard_map(
        per_device, mesh=mesh, in_specs=placed, out_specs=P("grp", "row", "col"), check_vma=False
    )
```

profile of v0, /device:TPU:0, one launch (start us, length us, event | category | flops | bytes accessed | tf_op | source)
XLA Modules:
  0.0 448.0 jit_solution(10581064769501468559)
XLA Ops:
  6.5 0.0 all-gather.4.cloned.1.call-start
  6.5 0.7 all-gather.4.cloned.1.call-update
  7.3 0.0 all-gather.6.cloned.1.call-start
  7.3 0.7 all-gather.6.cloned.1.call-update
  8.0 0.0 all-reduce.2.cloned.1.call-start
  8.1 32.1 %all-gather.4.cloned.1.call-done = bf16[3000,512]{1,0:T(8,128)(2,1)} async-done(((bf16[3000,128]{1,0:T(8,128)(2,1)}), bf16[3000,512]{1,0:T(8,128)(2,1)}) %all-gather.4.cloned.1.call-update) | async-done | bytes 3072016 | tf_op jit(solution)/shard_map/all_gather | solution.py:11
  40.1 25.8 %fusion.45 = bf16[2,3000,512,1]{2,1,3,0:T(8,128)(2,1)} fusion(bf16[2,3000,3000]{2,1,0:T(8,128)(2,1)} %param.5, bf16[3000,512]{1,0:T(8,128)(2,1)} %all-gather.4.cloned.1.call-done), kind=kOutput, calls=%fused_computation.5.clone.clone.clone.1 | convolution fusion | flops 18435072000 | bytes 45216000 | tf_op jit(solution)/shard_map/pij,jv->piv/dot_general | solution.py:14
  66.0 189.1 %all-gather.6.cloned.1.call-done = bf16[12000,500]{1,0:T(8,128)(2,1)} async-done(((bf16[3000,500]{1,0:T(8,128)(2,1)}), bf16[12000,500]{1,0:T(8,128)(2,1)}) %all-gather.6.cloned.1.call-update) | async-done | bytes 12000016 | tf_op jit(solution)/shard_map/all_gather | solution.py:12
  255.1 19.1 %fusion.17 = bf16[2,512,4,500]{1,3,2,0:T(8,128)(2,1)} fusion(bf16[4,3000,500,1]{2,1,0,3:T(8,128)(2,1)} %bitcast.58, bf16[2,3000,512,1]{2,1,3,0:T(8,128)(2,1)} %fusion.45), kind=kOutput, calls=%fused_computation.12 | convolution fusion | flops 12290048000 | bytes 22240000 | tf_op jit(solution)/shard_map/cio,piv->pcov/dot_general | solution.py:17
  274.2 0.0 copy-start
  274.2 0.0 copy-start.1
  274.2 7.8 %copy.10 = bf16[2,512,4,500]{3,2,1,0:T(4,128)(2,1)} copy(bf16[2,512,4,500]{1,3,2,0:T(8,128)(2,1)} %fusion.17) | data formatting | bytes 8192000
  282.0 0.0 all-reduce.2.cloned.1.call-update
  282.0 0.0 copy-done
  282.1 0.1 sub.19
  282.1 0.0 copy-done.1
  282.1 2.8 broadcast_subtract_fusion
  285.0 106.6 %all-reduce.2.cloned.1.call-done = bf16[2,4,500,512]{2,1,3,0:T(4,128)(2,1)} async-done(((bf16[2,4,500,512]{2,1,3,0:T(4,128)(2,1)}), bf16[2,4,500,512]{2,1,3,0:T(4,128)(2,1)}) %all-reduce.2.cloned.1.call-update) | async-done | bytes 4096016 | tf_op jit(solution)/shard_map/psum | solution.py:18
  391.5 5.5 %fusion = bf16[2,4,500,512]{2,1,3,0:T(4,128)(2,1)S(1)} fusion(bf16[2,4,500,512]{2,1,3,0:T(4,128)(2,1)} %all-reduce.2.cloned.1.call-done, f32[4,500,512]{1,0,2:T(4,128)} %broadcast_subtract_fusion), kind=kLoop, calls=%fused_computation.3 | loop fusion | flops 6144000 | bytes 12288000 | tf_op jit(solution)/shard_map/convert_element_type | solution.py:20
  397.1 16.8 %fusion.41 = bf16[2,3000,512]{2,1,0:T(8,128)(2,1)} fusion(bf16[4,3000,500,1]{2,1,0,3:T(8,128)(2,1)} %bitcast.59, bf16[2,4,500,512]{2,1,3,0:T(4,128)(2,1)S(1)} %fusion), kind=kOutput, calls=%fused_computation.6.clone.1 | convolution fusion | flops 12291072000 | bytes 22240000 | tf_op jit(solution)/shard_map/cio,pcov->piv/dot_general | solution.py:21
  413.9 27.6 %convolution_convert_fusion = bf16[2,3000,3000]{2,1,0:T(8,128)(2,1)} fusion(bf16[3000,512]{1,0:T(8,128)(2,1)} %all-gather.4.cloned.1.call-done, bf16[2,3000,512]{2,1,0:T(8,128)(2,1)} %fusion.41), kind=kOutput, calls=%fused_computation | convolution fusion | flops 18449999872 | bytes 45216000 | tf_op jit(solution)/shard_map/piv,jv->pij/dot_general | solution.py:24
Async XLA Ops:
  6.5 33.6 %all-gather.4.cloned.1.call-start = ((), (), s32[]{:S(2)}) async-start(), calls=%async_computation | async-start | bytes 3840000 | tf_op jit(solution)/shard_map/all_gather | solution.py:11
  7.3 247.8 %all-gather.6.cloned.1.call-start = ((), (), s32[]{:S(2)}) async-start(), calls=%async_computation.2 | async-start | bytes 15360000 | tf_op jit(solution)/shard_map/all_gather | solution.py:12
  8.0 383.5 %all-reduce.2.cloned.1.call-start = ((), (), s32[]{:S(2)}) async-start(), calls=%async_computation.1 | async-start | bytes 8388608 | tf_op jit(solution)/shard_map/psum | solution.py:18
  274.2 7.9 %copy-start = (f32[2000]{0:T(1024)S(1)}, f32[2000]{0:T(1024)}, u32[]{:S(2)}) copy-start(f32[2000]{0:T(1024)} %param.8) | copy-start | bytes 24004
  274.2 8.0 %copy-start.1 = (f32[512]{0:T(512)S(1)}, f32[512]{0:T(512)}, u32[]{:S(2)}) copy-start(f32[512]{0:T(512)} %param.9) | copy-start | bytes 6148
Sparse Core Ops, SparseCore 0:
  8.9 31.1 all-gather.3
  41.7 213.3 all-gather.5
  282.2 109.3 all-reduce.1
where the time goes:
time: 448 us
  waiting for transfers between devices  329 us (73%)
  matrix products  89.4 us (20%)
  between operations  13.1 us (3%)
  other arithmetic  8.38 us (2%)
  local copies, waits for them, and re-layouts  7.93 us (2%)
    all_gather x1, waiting for transfers between devices, per_device(): occ_parts = lax.all_gather(occ_coeffs, 'col')  189 us
    psum x1, waiting for transfers between devices, per_device(): coupling = lax.psum(part, ('row', 'col'))  107 us
    all_gather x1, waiting for transfers between devices, per_device(): vir_rows = lax.all_gather(vir_coeffs, 'row', axis=1, tiled=True)  32.1 us
    dot_general x1, matrix products, per_device(): jnp.einsum('piv,jv->pij', mixed, vir_rows, preferred_element_type=F32)  27.6 us
    dot_general x1, matrix products, per_device(): jnp.einsum('pij,jv->piv', perturbation, vir_rows, preferred_element_type=...  25.8 us
    dot_general x1, matrix products, per_device(): jnp.einsum('cio,piv->pcov', occ_parts, image, preferred_element_type=F32)  19.1 us
    dot_general x1, matrix products, per_device(): jnp.einsum('cio,pcov->piv', occ_parts, response, preferred_element_type=F32)  16.8 us
  transfers between devices with their start and end apart: 3, of which 3 were waited for; matrix products, arithmetic and copies ran while one was open for 6% of the time, Pallas kernels for 0%

commit v1 on v0

--- a/solution.py
+++ b/solution.py
@@ -15,7 +15,8 @@
         BF16
     )
     part = jnp.einsum("cio,piv->pcov", occ_parts, image, preferred_element_type=F32).astype(BF16)
-    coupling = lax.psum(part, ("row", "col"))
+    expand_results = lambda content: lax.psum(lax.psum(content, "col"), "row")
+    coupling = expand_results(part)
     gaps = occ_energies.reshape(cols, width)[:, :, None] - vir_energies[None, None, :]
     response = (coupling.astype(F32) / gaps[None]).astype(BF16)
     mixed = jnp.einsum("cio,pcov->piv", occ_parts, response, preferred_element_type=F32).astype(

time: 448 us -> 579 us (1.29)
  waiting for transfers between devices: 329 us -> 459 us
    psum x1 -> x2, waiting for transfers between devices: 107 us -> 237 us  [per_device(): expand_results = lambda content: lax.psum(lax.psum(content, 'col'), 'row')]
  transfers between devices with their start and end apart: 3 -> 4, of which waited for: 3 -> 4; matrix products, arithmetic and copies ran while one was open for 6% -> 5% of each run, Pallas kernels for 0% -> 0%
where the time goes in v1:
time: 579 us
  waiting for transfers between devices  459 us (79%)
  matrix products  89.4 us (15%)
  between operations  13.1 us (2%)
  other arithmetic  8.39 us (1%)
  local copies, waits for them, and re-layouts  7.9 us (1%)
    psum x2, waiting for transfers between devices, per_device(): expand_results = lambda content: lax.psum(lax.psum(content, 'col'), 'row')  237 us
    all_gather x1, waiting for transfers between devices, per_device(): occ_parts = lax.all_gather(occ_coeffs, 'col')  189 us
    all_gather x1, waiting for transfers between devices, per_device(): vir_rows = lax.all_gather(vir_coeffs, 'row', axis=1, tiled=True)  32.1 us
    dot_general x1, matrix products, per_device(): jnp.einsum('piv,jv->pij', mixed, vir_rows, preferred_element_type=F32)  27.6 us
    dot_general x1, matrix products, per_device(): jnp.einsum('pij,jv->piv', perturbation, vir_rows, preferred_element_type=...  25.8 us
    dot_general x1, matrix products, per_device(): jnp.einsum('cio,piv->pcov', occ_parts, image, preferred_element_type=F32)  19.1 us
    dot_general x1, matrix products, per_device(): jnp.einsum('cio,pcov->piv', occ_parts, response, preferred_element_type=F32)  16.8 us
  transfers between devices with their start and end apart: 4, of which 4 were waited for; matrix products, arithmetic and copies ran while one was open for 5% of the time, Pallas kernels for 0%

profile of v1, /device:TPU:0, one launch (start us, length us, event | category | flops | bytes accessed | tf_op | source)
XLA Modules:
  0.0 578.6 jit_solution(4163890639878657360)
XLA Ops:
  6.5 0.0 all-gather.4.cloned.1.call-start
  6.5 0.7 all-gather.4.cloned.1.call-update
  7.3 0.0 all-gather.6.cloned.1.call-start
  7.3 0.7 all-gather.6.cloned.1.call-update
  8.0 0.0 all-reduce.3.cloned.1.call-start
  8.1 32.1 %all-gather.4.cloned.1.call-done = bf16[3000,512]{1,0:T(8,128)(2,1)} async-done(((bf16[3000,128]{1,0:T(8,128)(2,1)}), bf16[3000,512]{1,0:T(8,128)(2,1)}) %all-gather.4.cloned.1.call-update) | async-done | bytes 3072016 | tf_op jit(solution)/shard_map/all_gather | solution.py:11
  40.1 25.8 %fusion.45 = bf16[2,3000,512,1]{2,1,3,0:T(8,128)(2,1)} fusion(bf16[2,3000,3000]{2,1,0:T(8,128)(2,1)} %param.5, bf16[3000,512]{1,0:T(8,128)(2,1)} %all-gather.4.cloned.1.call-done), kind=kOutput, calls=%fused_computation.5.clone.clone.clone.1 | convolution fusion | flops 18435072000 | bytes 45216000 | tf_op jit(solution)/shard_map/pij,jv->piv/dot_general | solution.py:14
  66.0 189.1 %all-gather.6.cloned.1.call-done = bf16[12000,500]{1,0:T(8,128)(2,1)} async-done(((bf16[3000,500]{1,0:T(8,128)(2,1)}), bf16[12000,500]{1,0:T(8,128)(2,1)}) %all-gather.6.cloned.1.call-update) | async-done | bytes 12000016 | tf_op jit(solution)/shard_map/all_gather | solution.py:12
  255.1 19.1 %fusion.17 = bf16[2,512,4,500]{1,3,2,0:T(8,128)(2,1)} fusion(bf16[4,3000,500,1]{2,1,0,3:T(8,128)(2,1)} %bitcast.58, bf16[2,3000,512,1]{2,1,3,0:T(8,128)(2,1)} %fusion.45), kind=kOutput, calls=%fused_computation.12 | convolution fusion | flops 12290048000 | bytes 22240000 | tf_op jit(solution)/shard_map/cio,piv->pcov/dot_general | solution.py:17
  274.2 7.8 %copy.10 = bf16[2,512,4,500]{3,2,1,0:T(4,128)(2,1)} copy(bf16[2,512,4,500]{1,3,2,0:T(8,128)(2,1)} %fusion.17) | data formatting | bytes 8192000
  282.0 0.0 copy-start
  282.0 0.0 copy-start.1
  282.0 0.0 all-reduce.3.cloned.1.call-update
  282.0 0.2 all-reduce.5.cloned.1.call-start
  282.2 153.1 %all-reduce.3.cloned.1.call-done = bf16[2,4,500,512]{2,1,3,0:T(4,128)(2,1)} async-done(((bf16[2,4,500,512]{2,1,3,0:T(4,128)(2,1)}), bf16[2,4,500,512]{2,1,3,0:T(4,128)(2,1)}) %all-reduce.3.cloned.1.call-update) | async-done | bytes 4096016 | tf_op jit(solution)/shard_map/psum | solution.py:18
  435.3 0.0 all-reduce.5.cloned.1.call-update
  435.4 0.0 copy-done
  435.4 0.1 sub.19
  435.5 0.0 copy-done.1
  435.5 2.8 broadcast_subtract_fusion
  438.3 83.7 %all-reduce.5.cloned.1.call-done = bf16[2,4,500,512]{2,1,3,0:T(4,128)(2,1)} async-done(((bf16[2,4,500,512]{2,1,3,0:T(4,128)(2,1)}), bf16[2,4,500,512]{2,1,3,0:T(4,128)(2,1)}) %all-reduce.5.cloned.1.call-update) | async-done | bytes 4096016 | tf_op jit(solution)/shard_map/psum | solution.py:18
  522.1 5.5 fusion
  527.6 16.8 %fusion.41 = bf16[2,3000,512]{2,1,0:T(8,128)(2,1)} fusion(bf16[4,3000,500,1]{2,1,0,3:T(8,128)(2,1)} %bitcast.59, bf16[2,4,500,512]{2,1,3,0:T(4,128)(2,1)S(1)} %fusion), kind=kOutput, calls=%fused_computation.6.clone.1 | convolution fusion | flops 12291072000 | bytes 22240000 | tf_op jit(solution)/shard_map/cio,pcov->piv/dot_general | solution.py:22
  544.4 27.6 %convolution_convert_fusion = bf16[2,3000,3000]{2,1,0:T(8,128)(2,1)} fusion(bf16[3000,512]{1,0:T(8,128)(2,1)} %all-gather.4.cloned.1.call-done, bf16[2,3000,512]{2,1,0:T(8,128)(2,1)} %fusion.41), kind=kOutput, calls=%fused_computation | convolution fusion | flops 18449999872 | bytes 45216000 | tf_op jit(solution)/shard_map/piv,jv->pij/dot_general | solution.py:25
Async XLA Ops:
  6.5 33.6 %all-gather.4.cloned.1.call-start = ((), (), s32[]{:S(2)}) async-start(), calls=%async_computation | async-start | bytes 3840000 | tf_op jit(solution)/shard_map/all_gather | solution.py:11
  7.3 247.8 %all-gather.6.cloned.1.call-start = ((), (), s32[]{:S(2)}) async-start(), calls=%async_computation.3 | async-start | bytes 15360000 | tf_op jit(solution)/shard_map/all_gather | solution.py:12
  8.0 427.3 %all-reduce.3.cloned.1.call-start = ((), (), s32[]{:S(2)}) async-start(), calls=%async_computation.1 | async-start | bytes 8388608 | tf_op jit(solution)/shard_map/psum | solution.py:18
  282.0 153.4 %copy-start = (f32[2000]{0:T(1024)S(1)}, f32[2000]{0:T(1024)}, u32[]{:S(2)}) copy-start(f32[2000]{0:T(1024)} %param.8) | copy-start | bytes 24004
  282.0 153.5 %copy-start.1 = (f32[512]{0:T(512)S(1)}, f32[512]{0:T(512)}, u32[]{:S(2)}) copy-start(f32[512]{0:T(512)} %param.9) | copy-start | bytes 6148
  282.0 240.0 %all-reduce.5.cloned.1.call-start = ((), (), s32[]{:S(2)}) async-start(), calls=%async_computation.2 | async-start | bytes 8388608 | tf_op jit(solution)/shard_map/psum | solution.py:18
Sparse Core Ops, SparseCore 0:
  8.9 31.1 all-gather.3
  41.7 213.3 all-gather.5
  282.1 153.1 all-reduce.2
  437.6 84.4 all-reduce.4
